TPU v7x, 32 devices: a whole 2x2x4 slice. The times are simulated.
32 devices in a mesh: tok: 4 (over z), out: 4 (over x, core), grp: 2 (over y).
Axes of the slice: x: 2, y: 2, z: 4, core: 2. Of those that a mesh axis runs over, the one named last changes fastest.
Arguments:
- activations: bfloat16 [1024, 2, 2048], P(('tok', 'grp'), None, 'out'), may hold values from -16 to 16
- out_grads: bfloat16 [1024, 2, 2048], P(('tok', 'grp'), None, 'out'), may hold values from -16 to 16
- weight: bfloat16 [2, 2048, 4096], P(None, 'out'), may hold values from -0.09375 to 0.09375
Outputs:
- update: bfloat16 [4096, 2, 2048], P(('tok', 'grp'), None, 'out')
- input_grad: bfloat16 [1024, 2, 2048], P(('tok', 'grp'), None, 'out')
All inputs are finite; a program needn't handle non-finite values.
Results may differ from a plain program's by a relative error of at most 0.0092.
Values may be sent and summed in bfloat16 or wider, within the bound.
A program may use at most 64 MiB of HBM per device.

v0:
```python
import math
import jax
import jax.numpy as jnp
from jax import lax
from jax.sharding import PartitionSpec as P

POWER = 3
DAMPING = 0.1
HIGH = lax.Precision.HIGHEST


def spread(piece):
    return lax.all_gather(piece, "out", axis=2, tiled=True)


def token_sums(maker, rows):
    return lax.psum_scatter(
        maker(jnp.int32(0), rows * lax.axis_size(("tok", "grp"))),
        ("tok", "grp"),
        scatter_dimension=0,
        tiled=True,
    )


def shared_rows(piece):
    return lax.all_gather(piece, ("tok", "grp"), axis=0, tiled=True)


def shared_total(vector):
    return lax.psum(vector, ("tok", "out", "grp"))


def diagonal_mask(rows, width, row_start, col_start):
    row_ids = row_start + lax.broadcasted_iota(jnp.int32, (rows, 1, width), 0)
    col_ids = col_start + lax.broadcasted_iota(jnp.int32, (rows, 1, width), 2)
    return jnp.where(row_ids == col_ids, 1.0, 0.0).astype(jnp.float32)


def multiply(left, right, gather_columns):
    row_band = spread(left)
    column_band = gather_columns(right)
    return jnp.einsum("rkj,jkc->rkc", row_band, column_band, preferred_element_type=jnp.float32)


def inverse_roots(tile, row_start, col_start, gather_columns, total):
    rows, count, width = tile.shape
    block = width * lax.axis_size("out")
    mask = diagonal_mask(rows, width, row_start, col_start)
    vector = jnp.ones((count, block), jnp.float32)
    image = vector
    for step in range(POWER):
        columns = lax.dynamic_slice_in_dim(vector, col_start, width, 1)
        part = jnp.einsum("rkc,kc->kr", tile, columns, precision=HIGH)
        placed = lax.dynamic_update_slice_in_dim(
            jnp.zeros((count, block), jnp.float32), part, row_start, 1
        )
        image = total(placed)
        if step + 1 < POWER:
            vector = image / jnp.sqrt(jnp.sum(image * image, axis=1, keepdims=True))
    scale = jnp.sum(vector * image, axis=1) / jnp.sum(vector * vector, axis=1)
    start = tile / scale[None, :, None]
    start_low = start.astype(jnp.bfloat16)
    first_low = ((3.0 * mask - start) / 2.0).astype(jnp.bfloat16)
    square_low = multiply(first_low, first_low, gather_columns).astype(jnp.bfloat16)
    moved = multiply(square_low, start_low, gather_columns)
    second_low = ((3.0 * mask - moved) / 2.0).astype(jnp.bfloat16)
    roots = multiply(first_low, second_low, gather_columns) / jnp.sqrt(scale)[None, :, None]
    return roots.astype(jnp.bfloat16)


def local(activations, out_grads, weight):
    tok_dev, blocks, width = activations.shape
    block = width * lax.axis_size("out")
    token_count = tok_dev * lax.axis_size("tok") * lax.axis_size("grp")
    col_start = lax.axis_index("out") * width
    local_sides = jnp.concatenate([activations, out_grads], axis=1)
    whole_sides = spread(local_sides)
    grads_whole = whole_sides[:, blocks:, :]
    weight_rows = weight.reshape(blocks, width, blocks, block)
    input_grad = jnp.einsum(
        "tjq,bcjq->tbc", grads_whole, weight_rows, preferred_element_type=jnp.float32
    ).astype(jnp.bfloat16)
    rows = block // (lax.axis_size("tok") * lax.axis_size("grp"))
    row_start = lax.axis_index(("tok", "grp")) * rows

    def shared_terms(start, span):
        return jnp.einsum(
            "tkr,tkc->rkc", whole_sides, local_sides, preferred_element_type=jnp.float32
        )

    sums = token_sums(shared_terms, rows)
    tile = sums / token_count + DAMPING * diagonal_mask(rows, width, row_start, col_start)
    roots = inverse_roots(tile, row_start, col_start, shared_rows, shared_total)
    bands = shared_rows(roots)
    whitened = jnp.einsum(
        "tkj,jkc->tkc", whole_sides, bands, preferred_element_type=jnp.float32
    ).astype(jnp.bfloat16)
    acts_whole = spread(whitened[:, :blocks, :]).reshape(tok_dev, blocks * block)
    grads_low = whitened[:, blocks:, :]
    owned_acts = lax.all_to_all(acts_whole, ("tok", "grp"), split_axis=1, concat_axis=0, tiled=True)
    update = jnp.einsum(
        "ta,tbc->abc",
        owned_acts,
        lax.all_gather(grads_low, ("tok", "grp"), axis=0, tiled=True),
        preferred_element_type=jnp.float32,
    )
    update = (update / math.sqrt(token_count)).astype(jnp.bfloat16)
    return (update, input_grad)


def token_space_whiten(sides, cols):
    tokens, block = sides.shape
    gram = jnp.einsum("tc,uc->tu", sides, sides, preferred_element_type=jnp.float32) / tokens
    ray_0 = jnp.sum(sides.astype(jnp.float32), axis=1)
    ray_1 = jnp.sum(gram * ray_0[None, :], axis=1) + DAMPING * ray_0
    ray_2 = jnp.sum(gram * ray_1[None, :], axis=1) + DAMPING * ray_1
    dots = [
        jnp.sum(ray_0 * ray_0),
        jnp.sum(ray_0 * ray_1),
        jnp.sum(ray_1 * ray_1),
        jnp.sum(ray_1 * ray_2),
        jnp.sum(ray_2 * ray_2),
    ]

    def moment(power):
        total = DAMPING**power * block
        for i in range(power):
            total = total + DAMPING ** (power - 1 - i) * dots[i] / tokens
        return total

    scale = moment(2 * POWER - 1) / moment(2 * POWER - 2)
    low = (gram / scale).astype(jnp.bfloat16)
    shift = DAMPING / scale

    def apply(value):
        product = jnp.einsum(
            "tu,uc->tc", low, value.astype(jnp.bfloat16), preferred_element_type=jnp.float32
        )
        return product + shift * value

    def first(value):
        return (3.0 * value - apply(value)) / 2.0

    head = first(cols.astype(jnp.float32))
    tail = first(first(apply(head)))
    return ((3.0 * head - tail) / 2.0 / jnp.sqrt(scale)).astype(jnp.bfloat16)


def planes(activations, out_grads, weight):
    tok_dev, blocks, width = activations.shape
    count = 2 * blocks
    tok, grp, out = (lax.axis_size(name) for name in ("tok", "grp", "out"))
    block = width * out
    token_count = tok_dev * tok * grp
    part = width // grp
    local_sides = jnp.concatenate([activations, out_grads], axis=1)
    pieces = jnp.swapaxes(local_sides, 0, 1)
    mine = lax.all_to_all(pieces, "tok", split_axis=0, concat_axis=0, tiled=True)
    mine = mine.reshape(tok * tok_dev, width)
    whole = lax.all_gather(mine, ("grp", "out"), axis=0, tiled=False)
    whole = whole.reshape(grp, out, tok * tok_dev, width)
    sides = jnp.transpose(whole, (0, 2, 1, 3)).reshape(token_count, block)
    start = lax.axis_index("out") * width + lax.axis_index("grp") * part
    cols = lax.dynamic_slice_in_dim(sides, start, part, 1)
    whitened = token_space_whiten(sides, cols)
    spread_low = lax.all_gather(whitened, ("tok", "grp"), axis=0, tiled=False)
    spread_low = spread_low.reshape(count, grp, token_count, part)
    grads_low = spread_low[blocks:]
    row = lax.axis_index(("tok", "grp"))
    own = lax.dynamic_index_in_dim(spread_low, row // out, 0, keepdims=False)
    owner = lax.rem(row, out) == lax.axis_index("out")
    acts_low = lax.psum(jnp.where(owner, own, jnp.zeros_like(own)), "out")
    update = jnp.einsum("yta,bxtc->yabxc", acts_low, grads_low, preferred_element_type=jnp.float32)
    update = (update / math.sqrt(token_count)).astype(jnp.bfloat16).reshape(width, blocks, width)
    grads_whole = spread(out_grads)
    weight_rows = weight.reshape(blocks, width, blocks, block)
    input_grad = jnp.einsum(
        "tjq,bcjq->tbc", grads_whole, weight_rows, preferred_element_type=jnp.float32
    ).astype(jnp.bfloat16)
    return (update, input_grad)


def solution(mesh):
    in_specs = (
        P(("tok", "grp"), None, "out"),
        P(("tok", "grp"), None, "out"),
        P(None, "out", None),
    )
    out_specs = (P(("tok", "grp"), None, "out"), P(("tok", "grp"), None, "out"))

    def body(activations, out_grads, weight):
        blocks = activations.shape[1]
        tok, grp, out = (mesh.shape[name] for name in ("tok", "grp", "out"))
        fits = tok == 2 * blocks and tok * grp == blocks * out
        return (planes if fits else local)(activations, out_grads, weight)

    return jax.shard_map(body, mesh=mesh, in_specs=in_specs, out_specs=out_specs, check_vma=False)
```

profile of v0, /device:TPU:0, one launch (start us, length us, event | category | flops | bytes accessed | tf_op | source)
XLA Modules:
  0.0 237.2 jit_solution(17187461038520449811)
XLA Ops:
  7.2 0.0 all-gather.5.cloned.1.call-start
  7.2 1.0 copy.28
  8.2 0.0 copy-start.4
  8.2 1.1 copy.27
  9.3 20.7 %all_to_all.5 = bf16[4,128,512]{2,1,0:T(8,128)(2,1)} all-to-all(bf16[4,128,512]{2,1,0:T(8,128)(2,1)S(1)} %maximum_bitcast_fusion), channel_id=1, replica_groups=mesh['tok'=4,'out'=4,'grp'=2] {'tok'}, dimensions={0} | all-to-all | bytes 1048576 | tf_op jit(solution)/shard_map/all_to_all | solution.py:158
  30.1 0.0 all-gather.5.cloned.1.call-update
  30.1 0.0 all-gather.9.cloned.1.call-start
  30.2 35.8 %all-gather.5.cloned.1.call-done = bf16[8,512,512]{2,1,0:T(8,128)(2,1)} async-done(((bf16[1,512,512]{2,1,0:T(8,128)(2,1)}), bf16[8,512,512]{2,1,0:T(8,128)(2,1)}) %all-gather.5.cloned.1.call-update) | async-done | bytes 4194320 | tf_op jit(solution)/shard_map/all_gather | solution.py:160
  66.0 0.0 copy-start.1
  66.0 3.0 %convert_reduce_fusion = f32[2,512]{1,0:T(2,128)S(1)} fusion(bf16[2,512,4,512]{3,1,2,0:T(8,128)(2,1)} %bitcast.45), kind=kLoop, calls=%fused_computation.3 | loop fusion | flops 4193280 | bytes 4198400 | tf_op jit(solution)/shard_map/reduce_sum | solution.py:114
  68.9 0.5 copy-done.1
  69.4 3.2 %copy.29 = bf16[2,512,4,512]{3,2,1,0:T(4,128)(2,1)S(1)} copy(bf16[2,512,4,512]{3,1,2,0:T(8,128)(2,1)S(1)} %bitcast.46) | data formatting | bytes 8388608 | tf_op jit(solution)/shard_map/transpose | solution.py:162
  72.6 0.0 copy-done.4
  72.7 0.6 multiply_reduce_fusion.6
  73.3 1.4 copy.42
  74.7 0.0 copy-start.2
  74.7 4.5 %multiply_reduce_fusion.1 = (f32[1024]{0:T(1024)S(1)}, f32[1024,1024]{0,1:T(8,128)S(1)}) fusion(f32[1024]{0:T(1024)S(1)} %broadcast_multiply_fusion.1, bf16[1024,2048]{1,0:T(8,128)(2,1)S(1)} %bitcast.48), kind=kOutput, calls=%fused_computation.6 | convolution fusion | flops 4297063424 | bytes 8396800 | tf_op jit(solution)/shard_map/tc,uc->tu/dot_general | solution.py:113
  79.2 0.0 copy-done.2
  79.2 0.0 copy-start
  79.3 1.9 copy-done
  81.2 0.3 multiply_reduce_fusion
  81.5 0.6 multiply_reduce_fusion.2
  87.7 2.8 %divide_convert_fusion = bf16[1024,1024]{0,1:T(8,128)(2,1)S(1)} fusion(f32[1024,1024]{0,1:T(8,128)} %copy-done, f32[]{:T(128)S(6)} %div.88), kind=kLoop, calls=%fused_computation.4 | loop fusion | flops 3145728 | bytes 6291460 | tf_op jit(solution)/shard_map/convert_element_type | solution.py:132
  90.6 2.1 fusion.8
  92.8 0.8 convolution_add_fusion.2
  93.6 0.9 fusion.7
  94.5 1.8 fusion.10
  96.3 0.0 all-gather.9.cloned.1.call-update
  96.3 0.0 all-gather.7.cloned.1.call-start
  96.4 0.7 all-gather.7.cloned.1.call-update
  97.1 0.0 all-reduce.2.cloned.1.call-start
  97.1 72.0 %all-gather.9.cloned.1.call-done = bf16[8192,256]{1,0:T(8,128)(2,1)} async-done(((bf16[1024,256]{1,0:T(8,128)(2,1)}), bf16[8192,256]{1,0:T(8,128)(2,1)}) %all-gather.9.cloned.1.call-update) | async-done | bytes 4194320 | tf_op jit(solution)/shard_map/all_gather | solution.py:166
  169.1 1.3 constant_dynamic-slice_fusion
  170.4 0.5 copy.40
  170.9 1.0 select_bitcast_fusion
  172.0 0.0 all-reduce.2.cloned.1.call-update
  172.0 14.5 %all-gather.7.cloned.1.call-done = bf16[128,2,2048]{2,0,1:T(8,128)(2,1)} async-done(((bf16[128,2,512]{2,0,1:T(8,128)(2,1)}), bf16[128,2,2048]{2,0,1:T(8,128)(2,1)}) %all-gather.7.cloned.1.call-update) | async-done | bytes 1048592 | tf_op jit(solution)/shard_map/all_gather | solution.py:13
  186.5 0.0 copy-start.3
  186.5 6.7 %fusion.14 = bf16[128,2,512]{2,0,1:T(8,128)(2,1)S(1)} fusion(bf16[2,64,2,8,2048]{4,3,2,1,0:T(8,128)(2,1)} %bitcast.57, bf16[128,2,2048]{2,0,1:T(8,128)(2,1)} %all-gather.7.cloned.1.call-done), kind=kOutput, calls=%fused_computation.23 | convolution fusion | flops 1073872896 | bytes 9699328 | tf_op jit(solution)/shard_map/tjq,bcjq->tbc/dot_general | solution.py:177
  193.3 1.0 copy.35
  194.2 0.0 copy-done.3
  194.2 0.1 slice.9
  194.4 31.2 %all-reduce.2.cloned.1.call-done = bf16[2,1024,256]{1,2,0:T(8,128)(2,1)} async-done(((bf16[2,1024,256]{1,2,0:T(8,128)(2,1)}), bf16[2,1024,256]{1,2,0:T(8,128)(2,1)}) %all-reduce.2.cloned.1.call-update) | async-done | bytes 1048592 | tf_op jit(solution)/shard_map/psum | solution.py:172
  225.6 2.5 %multiply_convert_fusion = bf16[2,256,2,2,256]{4,1,3,2,0:T(8,128)(2,1)S(1)} fusion(bf16[2,2,1024,256,1]{3,2,1,0,4:T(8,128)(2,1)S(1)} %bitcast.51, bf16[2,1024,256]{1,2,0:T(8,128)(2,1)} %all-reduce.2.cloned.1.call-done), kind=kOutput, calls=%fused_computation.7 | convolution fusion | flops 1074790400 | bytes 4194304 | tf_op jit(solution)/shard_map/yta,bxtc->yabxc/dot_general | solution.py:173
  228.1 1.1 copy.38
  229.2 1.5 reshape.68
  (4 shorter events, 0.1 us)
Async XLA Ops:
  7.2 58.8 %all-gather.5.cloned.1.call-start = ((), (), s32[]{:S(2)}) async-start(), calls=%async_computation.1 | async-start | bytes 4718592 | tf_op jit(solution)/shard_map/all_gather | solution.py:160
  8.2 64.5 %copy-start.4 = (bf16[128,2,512]{2,0,1:T(8,128)(2,1)}, bf16[128,2,512]{2,0,1:T(8,128)(2,1)S(1)}, u32[]{:S(2)}) copy-start(bf16[128,2,512]{2,0,1:T(8,128)(2,1)S(1)} %copy.28) | copy-start | bytes 786436
  30.1 139.0 %all-gather.9.cloned.1.call-start = ((), (), s32[]{:S(2)}) async-start(), calls=%async_computation.4 | async-start | bytes 4718592 | tf_op jit(solution)/shard_map/all_gather | solution.py:166
  66.0 3.4 %copy-start.1 = (bf16[8,512,512]{2,1,0:T(8,128)(2,1)S(1)}, bf16[8,512,512]{2,1,0:T(8,128)(2,1)}, u32[]{:S(2)}) copy-start(bf16[8,512,512]{2,1,0:T(8,128)(2,1)} %all-gather.5.cloned.1.call-done) | copy-start | bytes 12582916
  74.7 4.6 %copy-start.2 = (bf16[128,8,4,512]{3,1,2,0:T(8,128)(2,1)}, bf16[128,8,4,512]{3,1,2,0:T(8,128)(2,1)S(1)}, u32[]{:S(2)}) copy-start(bf16[128,8,4,512]{3,1,2,0:T(8,128)(2,1)S(1)} %copy.42) | copy-start | bytes 12582916
  79.2 2.0 copy-start
  96.3 90.2 %all-gather.7.cloned.1.call-start = ((), (), s32[]{:S(2)}) async-start(), calls=%async_computation.3 | async-start | bytes 1310720 | tf_op jit(solution)/shard_map/all_gather | solution.py:13
  97.1 128.6 %all-reduce.2.cloned.1.call-start = ((), (), s32[]{:S(2)}) async-start(), calls=%async_computation.2 | async-start | bytes 2097152 | tf_op jit(solution)/shard_map/psum | solution.py:172
  186.5 7.7 %copy-start.3 = (bf16[8192,256]{1,0:T(8,128)(2,1)S(1)}, bf16[8192,256]{1,0:T(8,128)(2,1)}, u32[]{:S(2)}) copy-start(bf16[8192,256]{1,0:T(8,128)(2,1)} %all-gather.9.cloned.1.call-done) | copy-start | bytes 12582916
Sparse Core Ops, SparseCore 0:
  30.2 35.6 all-gather.4
  96.4 72.6 all-gather.8
  171.2 15.2 all-gather.6
  189.3 36.2 all-reduce.1
where the time goes:
time: 238 us; the launch traced here: 237 us
  waiting for transfers between devices  154 us (65%)
  blocking collectives  20.7 us (9%)
  between operations  19.6 us (8%)
  matrix products  19.4 us (8%)
  local copies, waits for them, and re-layouts  14.6 us (6%)
  other arithmetic  8.42 us (4%)
    all_gather x1, waiting for transfers between devices, planes(): spread_low = lax.all_gather(whitened, ('tok', 'grp'), axis=0, tiled=False)  72 us
    all_gather x1, waiting for transfers between devices, planes(): whole = lax.all_gather(mine, ('grp', 'out'), axis=0, tiled=False)  35.8 us
    psum x1, waiting for transfers between devices, planes(): acts_low = lax.psum(jnp.where(owner, own, jnp.zeros_like(own)), 'out')  31.2 us
    all_to_all x1, blocking collectives, planes(): lax.all_to_all(pieces, 'tok', split_axis=0, concat_axis=0, tiled=True)  20.7 us
    all_gather x1, waiting for transfers between devices, spread(): return lax.all_gather(piece, 'out', axis=2, tiled=True)  14.5 us
    unnamed x18, local copies, waits for them, and re-layouts  9.98 us
    dot_general x1, matrix products, planes(): jnp.einsum('tjq,bcjq->tbc', grads_whole, weight_rows, preferred_element_t...  6.75 us
    dot_general x4, matrix products, apply(): jnp.einsum('tu,uc->tc', low, value.astype(jnp.bfloat16), preferred_elemen...  5.66 us
  transfers between devices with their start and end apart: 4, of which 4 were waited for; matrix products, arithmetic and copies ran while one was open for 5% of the time, Pallas kernels for 0%

commit v1 on v0

--- a/solution.py
+++ b/solution.py
@@ -10,7 +10,7 @@
 
 
 def spread(piece):
-    return lax.all_gather(piece, "out", axis=2, tiled=True)
+    return jnp.concatenate(lax.all_gather(piece, "out"), 2)
 
 
 def token_sums(maker, rows):

time: 238 us -> 219 us (0.920)
  waiting for transfers between devices: 154 us -> 133 us
  local copies, waits for them, and re-layouts: 14.6 us -> 17.4 us
    all_gather x1, waiting for transfers between devices: 14.5 us -> 0.02 us  [spread(): return jnp.concatenate(lax.all_gather(piece, 'out'), 2)]
    psum x1, waiting for transfers between devices: 31.2 us -> 27.4 us  [planes(): acts_low = lax.psum(jnp.where(owner, own, jnp.zeros_like(own)), 'out')]
    unnamed x18 -> x16, local copies, waits for them, and re-layouts: 9.98 us -> 9.88 us
  transfers between devices with their start and end apart: 4 -> 4, of which waited for: 4 -> 3; matrix products, arithmetic and copies ran while one was open for 5% -> 15% of each run, Pallas kernels for 0% -> 0%
where the time goes in v1:
time: 219 us
  waiting for transfers between devices  133 us (61%)
  blocking collectives  20.7 us (9%)
  between operations  19.9 us (9%)
  matrix products  19.1 us (9%)
  local copies, waits for them, and re-layouts  17.4 us (8%)
  other arithmetic  8.48 us (4%)
    all_gather x1, waiting for transfers between devices, planes(): spread_low = lax.all_gather(whitened, ('tok', 'grp'), axis=0, tiled=False)  69.8 us
    all_gather x1, waiting for transfers between devices, planes(): whole = lax.all_gather(mine, ('grp', 'out'), axis=0, tiled=False)  35 us
    psum x1, waiting for transfers between devices, planes(): acts_low = lax.psum(jnp.where(owner, own, jnp.zeros_like(own)), 'out')  27.4 us
    all_to_all x1, blocking collectives, planes(): lax.all_to_all(pieces, 'tok', split_axis=0, concat_axis=0, tiled=True)  20.7 us
    unnamed x16, local copies, waits for them, and re-layouts  9.88 us
    dot_general x1, matrix products, planes(): jnp.einsum('tjq,bcjq->tbc', grads_whole, weight_rows, preferred_element_t...  6.41 us
    dot_general x4, matrix products, apply(): jnp.einsum('tu,uc->tc', low, value.astype(jnp.bfloat16), preferred_elemen...  5.66 us
    dot_general x1, matrix products, token_space_whiten(): jnp.einsum('tc,uc->tu', sides, sides, preferred_element_type=jnp.float32)  4.53 us
  transfers between devices with their start and end apart: 4, of which 3 were waited for; matrix products, arithmetic and copies ran while one was open for 15% of the time, Pallas kernels for 0%

profile of v1, /device:TPU:0, one launch (start us, length us, event | category | flops | bytes accessed | tf_op | source)
XLA Modules:
  0.0 218.8 jit_solution(11139871494118409330)
XLA Ops:
  7.2 0.0 all-gather.6.cloned.1.call-start
  7.2 1.0 copy.27
  8.2 1.0 copy.28
  9.2 20.7 %all_to_all.5 = bf16[4,128,512]{2,1,0:T(8,128)(2,1)} all-to-all(bf16[4,128,512]{2,1,0:T(8,128)(2,1)S(1)} %maximum_bitcast_fusion), channel_id=1, replica_groups=mesh['tok'=4,'out'=4,'grp'=2] {'tok'}, dimensions={0} | all-to-all | bytes 1048576 | tf_op jit(solution)/shard_map/all_to_all | solution.py:158
  30.0 0.0 all-gather.6.cloned.1.call-update
  30.0 0.0 all-gather.10.cloned.1.call-start
  30.0 0.7 all-gather.10.cloned.1.call-update
  30.8 0.0 all-gather.8.cloned.1.call-start
  30.8 35.0 %all-gather.6.cloned.1.call-done = bf16[8,512,512]{2,1,0:T(8,128)(2,1)} async-done(((bf16[1,512,512]{2,1,0:T(8,128)(2,1)}), bf16[8,512,512]{2,1,0:T(8,128)(2,1)}) %all-gather.6.cloned.1.call-update) | async-done | bytes 4194320 | tf_op jit(solution)/shard_map/all_gather | solution.py:160
  65.8 0.0 copy-start.1
  65.8 3.0 %convert_reduce_fusion = f32[2,512]{1,0:T(2,128)S(1)} fusion(bf16[2,512,4,512]{3,1,2,0:T(8,128)(2,1)} %bitcast.49), kind=kLoop, calls=%fused_computation.3 | loop fusion | flops 4193280 | bytes 4198400 | tf_op jit(solution)/shard_map/reduce_sum | solution.py:114
  68.8 0.5 copy-done.1
  69.3 3.2 %copy.29 = bf16[2,512,4,512]{3,2,1,0:T(4,128)(2,1)S(1)} copy(bf16[2,512,4,512]{3,1,2,0:T(8,128)(2,1)S(1)} %bitcast.50) | data formatting | bytes 8388608 | tf_op jit(solution)/shard_map/transpose | solution.py:162
  72.5 0.6 multiply_reduce_fusion.6
  73.1 1.4 copy.42
  74.5 0.0 copy-start.2
  74.6 4.5 %multiply_reduce_fusion.1 = (f32[1024]{0:T(1024)S(1)}, f32[1024,1024]{0,1:T(8,128)S(1)}) fusion(f32[1024]{0:T(1024)S(1)} %broadcast_multiply_fusion.1, bf16[1024,2048]{1,0:T(8,128)(2,1)S(1)} %bitcast.52), kind=kOutput, calls=%fused_computation.6 | convolution fusion | flops 4297063424 | bytes 8396800 | tf_op jit(solution)/shard_map/tc,uc->tu/dot_general | solution.py:113
  79.1 0.0 copy-done.2
  79.1 0.0 copy-start
  79.1 1.9 copy-done
  81.1 0.3 multiply_reduce_fusion
  81.4 0.7 multiply_reduce_fusion.2
  88.0 2.8 %divide_convert_fusion = bf16[1024,1024]{0,1:T(8,128)(2,1)S(1)} fusion(f32[1024,1024]{0,1:T(8,128)} %copy-done, f32[]{:T(128)S(6)} %div.88), kind=kLoop, calls=%fused_computation.4 | loop fusion | flops 3145728 | bytes 6291460 | tf_op jit(solution)/shard_map/convert_element_type | solution.py:132
  90.9 2.1 fusion.8
  93.0 0.8 convolution_add_fusion.2
  93.8 0.9 fusion.7
  94.7 1.8 fusion.10
  96.5 0.0 all-gather.8.cloned.1.call-update
  96.6 0.0 all-reduce.2.cloned.1.call-start
  96.6 0.0 all-gather.10.cloned.1.call-done
  96.7 2.0 copy.53
  98.7 0.8 reshape.75
  99.5 69.8 %all-gather.8.cloned.1.call-done = bf16[8192,256]{1,0:T(8,128)(2,1)} async-done(((bf16[1024,256]{1,0:T(8,128)(2,1)}), bf16[8192,256]{1,0:T(8,128)(2,1)}) %all-gather.8.cloned.1.call-update) | async-done | bytes 4194320 | tf_op jit(solution)/shard_map/all_gather | solution.py:166
  169.4 1.3 constant_dynamic-slice_fusion
  170.6 0.5 copy.40
  171.2 1.0 select_bitcast_fusion
  172.2 0.0 all-reduce.2.cloned.1.call-update
  172.3 0.0 copy-start.3
  172.3 6.4 %fusion.14 = bf16[128,2,512]{2,0,1:T(8,128)(2,1)S(1)} fusion(bf16[128,2,2048,1]{2,0,1,3:T(8,128)(2,1)S(1)} %reshape.75, bf16[2,64,2,8,2048]{4,3,2,1,0:T(8,128)(2,1)} %bitcast.63), kind=kOutput, calls=%fused_computation.23 | convolution fusion | flops 1073872896 | bytes 9699328 | tf_op jit(solution)/shard_map/tjq,bcjq->tbc/dot_general | solution.py:177
  178.7 1.0 copy.35
  179.7 0.0 copy-done.3
  179.7 0.1 slice.9
  179.8 27.4 %all-reduce.2.cloned.1.call-done = bf16[2,1024,256]{1,2,0:T(8,128)(2,1)} async-done(((bf16[2,1024,256]{1,2,0:T(8,128)(2,1)}), bf16[2,1024,256]{1,2,0:T(8,128)(2,1)}) %all-reduce.2.cloned.1.call-update) | async-done | bytes 1048592 | tf_op jit(solution)/shard_map/psum | solution.py:172
  207.2 2.5 %multiply_convert_fusion = bf16[2,256,2,2,256]{4,1,3,2,0:T(8,128)(2,1)S(1)} fusion(bf16[2,2,1024,256,1]{3,2,1,0,4:T(8,128)(2,1)S(1)} %bitcast.56, bf16[2,1024,256]{1,2,0:T(8,128)(2,1)} %all-reduce.2.cloned.1.call-done), kind=kOutput, calls=%fused_computation.7 | convolution fusion | flops 1074790400 | bytes 4194304 | tf_op jit(solution)/shard_map/yta,bxtc->yabxc/dot_general | solution.py:173
  209.7 1.1 copy.38
  210.8 1.5 reshape.77
  (4 shorter events, 0.1 us)
Async XLA Ops:
  7.2 58.7 %all-gather.6.cloned.1.call-start = ((), (), s32[]{:S(2)}) async-start(), calls=%async_computation.1 | async-start | bytes 4718592 | tf_op jit(solution)/shard_map/all_gather | solution.py:160
  30.0 66.7 %all-gather.10.cloned.1.call-start = ((), (), s32[]{:S(2)}) async-start(), calls=%async_computation.4 | async-start | bytes 1310720 | tf_op jit(solution)/shard_map/all_gather | solution.py:13
  30.8 138.6 %all-gather.8.cloned.1.call-start = ((), (), s32[]{:S(2)}) async-start(), calls=%async_computation.3 | async-start | bytes 4718592 | tf_op jit(solution)/shard_map/all_gather | solution.py:166
  65.8 3.4 %copy-start.1 = (bf16[8,512,512]{2,1,0:T(8,128)(2,1)S(1)}, bf16[8,512,512]{2,1,0:T(8,128)(2,1)}, u32[]{:S(2)}) copy-start(bf16[8,512,512]{2,1,0:T(8,128)(2,1)} %all-gather.6.cloned.1.call-done) | copy-start | bytes 12582916
  74.5 4.6 %copy-start.2 = (bf16[128,8,4,512]{3,1,2,0:T(8,128)(2,1)}, bf16[128,8,4,512]{3,1,2,0:T(8,128)(2,1)S(1)}, u32[]{:S(2)}) copy-start(bf16[128,8,4,512]{3,1,2,0:T(8,128)(2,1)S(1)} %copy.42) | copy-start | bytes 12582916
  79.1 2.0 copy-start
  96.6 110.6 %all-reduce.2.cloned.1.call-start = ((), (), s32[]{:S(2)}) async-start(), calls=%async_computation.2 | async-start | bytes 2097152 | tf_op jit(solution)/shard_map/psum | solution.py:172
  172.3 7.4 %copy-start.3 = (bf16[8192,256]{1,0:T(8,128)(2,1)S(1)}, bf16[8192,256]{1,0:T(8,128)(2,1)}, u32[]{:S(2)}) copy-start(bf16[8192,256]{1,0:T(8,128)(2,1)} %all-gather.8.cloned.1.call-done) | copy-start | bytes 12582916
Sparse Core Ops, SparseCore 0:
  30.1 35.6 all-gather.5
  67.4 16.7 all-gather.9
  96.7 72.6 all-gather.7
  172.4 34.7 all-reduce.1
